TPU v7x, 512 devices: a whole 4x8x8 slice. The times are simulated.
512 devices in a mesh: row: 32 (over y, z_lo, core), col: 16 (over z_hi, x).
Axes of the slice: x: 4, y: 8, z: 8 (z_hi: 4, z_lo: 2; z = z_hi * 2 + z_lo), core: 2. Of those that a mesh axis runs over, the one named last changes fastest.
Arguments:
- residual: float32 [8192, 8192], P('row', 'col'), may hold values from -0.15625 to 0.15625
- direction: float32 [8192, 8192], P('row', 'col'), may hold values from -6 to 6
- ground_shift: float32 [1], replicated, may hold values from 1.6937256e-06 to 6.7749024e-06
- previous: float32 [1], replicated, may hold values from 3072 to 12288
Outputs:
- next_direction: float32 [8192, 8192], P('row', 'col')
- step_ratio: float32 [1], replicated
All inputs are finite; a program needn't handle non-finite values.
Results may differ from a plain program's by a relative error of at most 0.00015.
Values sent between devices are 32-bit elements; how exact they have to be, the bound alone decides.
No kernel may reach another device: no remote copies, remote signals or barrier semaphores. Data moves between devices by JAX's collectives and lax.ppermute only.
A program may use at most 64 MiB of HBM per device.

v0:
```python
import jax
import jax.numpy as jnp
from jax import lax
from jax.sharding import Mesh
from jax.sharding import PartitionSpec as P

COL = ("col_0", "col_1")
ROW = ("row_0", "row_1", "row_2")
ROW_COL = ("row_0", "row_1", "row_2", "col_0", "col_1")
PRECISE = lax.Precision.HIGHEST


def over_axes(array, axes):
    for axis in axes:
        array = lax.psum(array, axis)
    return array


def mixing_tables(devices):
    target = jnp.arange(devices, dtype=jnp.int32)[:, None]
    source = jnp.arange(devices, dtype=jnp.int32)[None, :]
    angles = jnp.pi * (target * source % (2 * devices)).astype(jnp.float32) / devices
    parity = jnp.where(source % 2 == 0, 1.0, -1.0).astype(jnp.float32)
    return (jnp.cos(angles), jnp.where(target > 0, jnp.sin(angles), parity))


def local_tables(extent, devices, device_index):
    length = extent * devices
    halfway = extent // 2
    position = jnp.arange(extent, dtype=jnp.int32)[:, None]
    steps_m = jnp.arange(halfway, dtype=jnp.int32)
    second_wave = jnp.where(device_index == 0, devices, 2 * devices - device_index)
    first_waves = 2 * devices * steps_m + device_index
    second_waves = 2 * devices * steps_m + second_wave

    def table_pair(wavenums):
        phases = wavenums[None, :] * (2 * position + 1) % (4 * length)
        angles = jnp.pi * phases.astype(jnp.float32) / (2 * length)
        scaling = jnp.where(wavenums == 0, jnp.sqrt(1.0 / length), jnp.sqrt(2.0 / length)).astype(
            jnp.float32
        )
        return (scaling[None, :] * jnp.cos(angles), scaling[None, :] * jnp.sin(angles))

    cos_one, sin_one = table_pair(first_waves)
    cos_two, sin_two = table_pair(second_waves)
    nonzero = (device_index > 0).astype(jnp.float32)
    tables = (
        cos_one,
        -nonzero * sin_one,
        nonzero * cos_two,
        jnp.where(device_index > 0, sin_two, cos_two),
    )
    return (tables, jnp.concatenate([first_waves, second_waves]))


def spread_forward(mix_cos, mix_sin):

    def combine(pieces):
        source = pieces[0]
        real_part = jnp.einsum("td,dab->tab", mix_cos, source, precision=PRECISE)
        imag_part = jnp.einsum("td,dab->tab", mix_sin, source, precision=PRECISE)
        return (real_part, imag_part)

    return combine


def spread_inverse(mix_cos, mix_sin):

    def combine(pieces):
        real_part = jnp.einsum("td,tab->dab", mix_cos, pieces[0], precision=PRECISE)
        imag_part = jnp.einsum("td,tab->dab", mix_sin, pieces[1], precision=PRECISE)
        return (real_part + imag_part,)

    return combine


def across_columns(arrays, combine):
    devices = lax.axis_size(COL)

    def handle(pieces):
        mixed = combine(pieces)
        return lax.all_to_all(mixed, COL, split_axis=0, concat_axis=0, tiled=True)

    shaped = tuple(
        (
            member.reshape((devices, member.shape[0] // devices) + member.shape[1:])
            for member in arrays
        )
    )
    result = handle(lax.all_to_all(shaped, COL, split_axis=0, concat_axis=0, tiled=True))
    return tuple((member.reshape((-1,) + member.shape[2:]) for member in result))


def across_rows(arrays, combine):
    devices = lax.axis_size(ROW)

    def handle(pieces):
        mixed = combine(pieces)
        return lax.all_to_all(mixed, ROW, split_axis=0, concat_axis=0, tiled=True)

    shaped = tuple(
        (
            member.reshape((devices, member.shape[0] // devices) + member.shape[1:])
            for member in arrays
        )
    )
    result = handle(lax.all_to_all(shaped, ROW, split_axis=0, concat_axis=0, tiled=True))
    return tuple((member.reshape((-1,) + member.shape[2:]) for member in result))


def body(residual, direction, ground_shift, previous):
    row_count = lax.axis_size(ROW)
    col_count = lax.axis_size(COL)
    row_index = lax.axis_index(ROW)
    col_index = lax.axis_index(COL)
    rows_here = residual.shape[0]
    cols_here = residual.shape[1]
    halfway_rows = rows_here // 2
    halfway_cols = cols_here // 2
    col_tables, col_waves = local_tables(cols_here, col_count, col_index)
    row_tables, row_waves = local_tables(rows_here, row_count, row_index)
    col_cos, col_sin = mixing_tables(col_count)
    row_cos, row_sin = mixing_tables(row_count)
    real_part, imag_part = across_columns((residual,), spread_forward(col_cos, col_sin))
    left_half = jnp.dot(real_part, col_tables[0], precision=PRECISE) + jnp.dot(
        imag_part, col_tables[1], precision=PRECISE
    )
    right_half = jnp.dot(real_part, col_tables[2], precision=PRECISE) + jnp.dot(
        imag_part, col_tables[3], precision=PRECISE
    )
    partial_spectrum = jnp.concatenate([left_half, right_half], axis=1)
    real_part, imag_part = across_rows((partial_spectrum,), spread_forward(row_cos, row_sin))
    upper_half = jnp.dot(row_tables[0].T, real_part, precision=PRECISE) + jnp.dot(
        row_tables[1].T, imag_part, precision=PRECISE
    )
    lower_half = jnp.dot(row_tables[2].T, real_part, precision=PRECISE) + jnp.dot(
        row_tables[3].T, imag_part, precision=PRECISE
    )
    spectrum = jnp.concatenate([upper_half, lower_half], axis=0)
    row_total = rows_here * row_count
    col_total = cols_here * col_count
    row_sine = jnp.sin(jnp.pi * row_waves.astype(jnp.float32) / (2 * row_total))
    col_sine = jnp.sin(jnp.pi * col_waves.astype(jnp.float32) / (2 * col_total))
    eigenvalue = 4.0 * (row_sine * row_sine)[:, None] + 4.0 * (col_sine * col_sine)[None, :]
    weight = 1.0 / (eigenvalue + ground_shift[0])
    scaled = weight * spectrum
    upper_half = scaled[:halfway_rows]
    lower_half = scaled[halfway_rows:]
    back_real = jnp.dot(row_tables[0], upper_half, precision=PRECISE) + jnp.dot(
        row_tables[2], lower_half, precision=PRECISE
    )
    back_imag = jnp.dot(row_tables[1], upper_half, precision=PRECISE) + jnp.dot(
        row_tables[3], lower_half, precision=PRECISE
    )
    partial_field = across_rows((back_real, back_imag), spread_inverse(row_cos, row_sin))[0]
    left_half = partial_field[:, :halfway_cols]
    right_half = partial_field[:, halfway_cols:]
    back_real = jnp.dot(left_half, col_tables[0].T, precision=PRECISE) + jnp.dot(
        right_half, col_tables[2].T, precision=PRECISE
    )
    back_imag = jnp.dot(left_half, col_tables[1].T, precision=PRECISE) + jnp.dot(
        right_half, col_tables[3].T, precision=PRECISE
    )
    precond = across_columns((back_real, back_imag), spread_inverse(col_cos, col_sin))[0]
    local_inner = jnp.sum(spectrum * scaled)
    inner_total = over_axes(local_inner, ROW_COL)
    step_ratio = inner_total / previous[0]
    return (precond + step_ratio * direction, jnp.reshape(step_ratio, (1,)))


def solution(mesh):
    finer = Mesh(mesh.devices.reshape(8, 2, 2, 4, 4), ("row_0", "row_1", "row_2", "col_0", "col_1"))
    return jax.shard_map(
        body,
        mesh=finer,
        in_specs=(P(ROW, COL), P(ROW, COL), P(), P()),
        out_specs=(P(ROW, COL), P()),
        check_vma=False,
    )
```

profile of v0, /device:TPU:8, one launch (start us, length us, event | category | flops | bytes accessed | tf_op | source)
XLA Modules:
  0.0 333.4 jit_solution(59591209044560012)
XLA Ops:
  0.6 28.6 %all_to_all.60 = f32[16,16,512]{2,1,0:T(8,128)S(1)} all-to-all(f32[16,16,512]{2,1,0:T(8,128)} %bitcast.57), channel_id=1, replica_groups=mesh['row_0'=8,'row_1'=2,'row_2'=2,'col_0'=4,'col_1'=4] {'col_0','col_1'}, dimensions={0} | all-to-all | bytes 1048576 | tf_op jit(solution)/shard_map/all_to_all | solution.py:90
  30.1 1.1 copy.34
  31.2 5.9 %all-to-all-start.1 = ((f32[16,16,512]{2,1,0:T(8,128)}), f32[16,16,512]{2,1,0:T(8,128)S(1)}, u32[]{:S(2)}, u32[]{:S(2)}) async-start(f32[16,16,512]{2,1,0:T(8,128)} %copy.34), calls=%async_computation.1 | async-start | bytes 1048576 | tf_op jit(solution)/shard_map/all_to_all | solution.py:82
  38.0 1.1 copy.37
  39.1 12.4 %all-to-all-done.1 = f32[16,16,512]{2,1,0:T(8,128)S(1)} async-done(((f32[16,16,512]{2,1,0:T(8,128)}), f32[16,16,512]{2,1,0:T(8,128)S(1)}, u32[]{:S(2)}, u32[]{:S(2)}) %all-to-all-start.1) | async-done | bytes 524320 | tf_op jit(solution)/shard_map/all_to_all | solution.py:82
  51.5 7.4 %all-to-all-start.2 = ((f32[16,16,512]{2,1,0:T(8,128)}), f32[16,16,512]{2,1,0:T(8,128)S(1)}, u32[]{:S(2)}, u32[]{:S(2)}) async-start(f32[16,16,512]{2,1,0:T(8,128)} %copy.37), calls=%async_computation.2 | async-start | bytes 1048576 | tf_op jit(solution)/shard_map/all_to_all | solution.py:82
  58.9 3.0 fusion.33
  61.9 2.9 fusion.30
  64.9 9.2 %all-to-all-done.2 = f32[16,16,512]{2,1,0:T(8,128)S(1)} async-done(((f32[16,16,512]{2,1,0:T(8,128)}), f32[16,16,512]{2,1,0:T(8,128)S(1)}, u32[]{:S(2)}, u32[]{:S(2)}) %all-to-all-start.2) | async-done | bytes 524320 | tf_op jit(solution)/shard_map/all_to_all | solution.py:82
  74.1 3.1 convolution_add_fusion.8
  77.2 3.6 %convolution_add_fusion.9 = f32[256,256]{0,1:T(8,128)S(1)} fusion(f32[256,256]{0,1:T(8,128)S(1)} %fusion.30, f32[256,512]{1,0:T(8,128)S(1)} %bitcast.61, f32[]{:T(128)S(6)} %neg.6, s32[512]{0:T(512)S(1)} %multiply_add_fusion, s32[256]{0:T(256)S(1)} %get-tuple-element.5, f32[256]{0:T(256)S(1)} %compare_select_fusion.4), kind=kOutput, calls=%fused_computation.11 | convolution fusion | flops 404815872 | bytes 1052676 | tf_op jit(solution)/shard_map/dot_general | solution.py:125
  81.0 25.2 %all_to_all.61 = f32[32,8,512]{2,1,0:T(8,128)S(1)} all-to-all(f32[32,8,512]{2,1,0:T(8,128)S(1)} %bitcast.56), channel_id=1, replica_groups=mesh['row_0'=8,'row_1'=2,'row_2'=2,'col_0'=4,'col_1'=4] {'row_0','row_1'..., dimensions={0} | all-to-all | bytes 1048576 | tf_op jit(solution)/shard_map/all_to_all | solution.py:107
  106.3 0.9 fusion.23
  107.2 1.1 copy.41
  108.3 4.7 %all-to-all-start.4 = ((f32[32,8,512]{2,1,0:T(8,128)}), f32[32,8,512]{2,1,0:T(8,128)S(1)}, u32[]{:S(2)}, u32[]{:S(2)}) async-start(f32[32,8,512]{2,1,0:T(8,128)} %copy.41), calls=%async_computation.4 | async-start | bytes 1048576 | tf_op jit(solution)/shard_map/all_to_all | solution.py:99
  113.7 0.9 fusion.21
  114.6 1.1 copy.44
  115.7 14.1 %all-to-all-done.4 = f32[32,8,512]{2,1,0:T(8,128)S(1)} async-done(((f32[32,8,512]{2,1,0:T(8,128)}), f32[32,8,512]{2,1,0:T(8,128)S(1)}, u32[]{:S(2)}, u32[]{:S(2)}) %all-to-all-start.4) | async-done | bytes 524320 | tf_op jit(solution)/shard_map/all_to_all | solution.py:99
  129.9 5.0 %all-to-all-start.5 = ((f32[32,8,512]{2,1,0:T(8,128)}), f32[32,8,512]{2,1,0:T(8,128)S(1)}, u32[]{:S(2)}, u32[]{:S(2)}) async-start(f32[32,8,512]{2,1,0:T(8,128)} %copy.44), calls=%async_computation.5 | async-start | bytes 1048576 | tf_op jit(solution)/shard_map/all_to_all | solution.py:99
  135.0 1.0 fusion.10
  136.0 1.0 fusion.12
  137.0 14.7 %all-to-all-done.5 = f32[32,8,512]{2,1,0:T(8,128)S(1)} async-done(((f32[32,8,512]{2,1,0:T(8,128)}), f32[32,8,512]{2,1,0:T(8,128)S(1)}, u32[]{:S(2)}, u32[]{:S(2)}) %all-to-all-start.5) | async-done | bytes 524320 | tf_op jit(solution)/shard_map/all_to_all | solution.py:99
  151.8 1.0 convolution_add_fusion.6
  152.8 1.0 convolution_add_fusion.7
  154.8 1.1 fusion.65
  155.9 1.9 fusion.1
  157.8 5.3 %all-to-all-start.6 = ((f32[32,8,512]{2,1,0:T(8,128)}), f32[32,8,512]{2,1,0:T(8,128)S(1)}, u32[]{:S(2)}, u32[]{:S(2)}) async-start(f32[32,8,512]{2,1,0:T(8,128)} %fusion.1), calls=%async_computation.6 | async-start | bytes 1048576 | tf_op jit(solution)/shard_map/all_to_all | solution.py:107
  163.1 1.1 fusion.63
  164.2 2.0 fusion
  166.2 13.7 %all-to-all-done.6 = f32[32,8,512]{2,1,0:T(8,128)S(1)} async-done(((f32[32,8,512]{2,1,0:T(8,128)}), f32[32,8,512]{2,1,0:T(8,128)S(1)}, u32[]{:S(2)}, u32[]{:S(2)}) %all-to-all-start.6) | async-done | bytes 524320 | tf_op jit(solution)/shard_map/all_to_all | solution.py:107
  179.8 5.0 %all-to-all-start.7 = ((f32[32,8,512]{2,1,0:T(8,128)}), f32[32,8,512]{2,1,0:T(8,128)S(1)}, u32[]{:S(2)}, u32[]{:S(2)}) async-start(f32[32,8,512]{2,1,0:T(8,128)} %fusion), calls=%async_computation.7 | async-start | bytes 1048576 | tf_op jit(solution)/shard_map/all_to_all | solution.py:107
  185.7 16.0 %all-to-all-done.7 = f32[32,8,512]{2,1,0:T(8,128)S(1)} async-done(((f32[32,8,512]{2,1,0:T(8,128)}), f32[32,8,512]{2,1,0:T(8,128)S(1)}, u32[]{:S(2)}, u32[]{:S(2)}) %all-to-all-start.7) | async-done | bytes 524320 | tf_op jit(solution)/shard_map/all_to_all | solution.py:107
  202.9 21.0 %all_to_all.62 = f32[32,8,512]{2,1,0:T(8,128)S(1)} all-to-all(f32[32,8,512]{2,1,0:T(8,128)S(1)} %copy.47), channel_id=1, replica_groups=mesh['row_0'=8,'row_1'=2,'row_2'=2,'col_0'=4,'col_1'=4] {'row_0','row_1'..., dimensions={0} | all-to-all | bytes 1048576 | tf_op jit(solution)/shard_map/all_to_all | solution.py:99
  223.9 2.6 fusion.29
  226.5 3.6 %convolution_add_fusion.5 = f32[256,512]{1,0:T(8,128)} fusion(f32[256,512]{1,0:T(8,128)S(1)} %fusion.29, f32[256]{0:T(256)S(1)} %compare_select_fusion.2, f32[]{:T(128)S(6)} %convert_element_type.56, s32[256]{0:T(256)S(1)} %get-tuple-element.4, s32[512]{0:T(512)S(1)} %multiply_add_fusion, f32[256,512]{1,0:T(8,128)S(1)} %bitcast.63), kind=kOutput, calls=%fused_computation.7 | convolution fusion | flops 404881408 | bytes 1314820 | tf_op jit(solution)/shard_map/dot_general | solution.py:158
  230.1 5.8 %all-to-all-start.9 = ((f32[16,16,512]{2,1,0:T(8,128)}), f32[16,16,512]{2,1,0:T(8,128)S(1)}, u32[]{:S(2)}, u32[]{:S(2)}) async-start(f32[16,16,512]{2,1,0:T(8,128)} %bitcast.17), calls=%async_computation.9 | async-start | bytes 1048576 | tf_op jit(solution)/shard_map/all_to_all | solution.py:90
  235.9 2.6 fusion.31
  238.6 3.8 %convolution_add_fusion.4 = f32[256,512]{1,0:T(8,128)} fusion(f32[256,512]{1,0:T(8,128)S(1)} %fusion.31, f32[256]{0:T(256)S(1)} %compare_select_fusion.2, s32[256]{0:T(256)S(1)} %get-tuple-element.4, s32[512]{0:T(512)S(1)} %multiply_add_fusion, pred[]{:T(512)S(6)} %gt.32, f32[256,512]{1,0:T(8,128)S(1)} %bitcast.65), kind=kOutput, calls=%fused_computation.6 | convolution fusion | flops 405012480 | bytes 1314817 | tf_op jit(solution)/shard_map/dot_general | solution.py:161
  242.3 9.1 %all-to-all-done.9 = f32[16,16,512]{2,1,0:T(8,128)S(1)} async-done(((f32[16,16,512]{2,1,0:T(8,128)}), f32[16,16,512]{2,1,0:T(8,128)S(1)}, u32[]{:S(2)}, u32[]{:S(2)}) %all-to-all-start.9) | async-done | bytes 524320 | tf_op jit(solution)/shard_map/all_to_all | solution.py:90
  251.5 6.7 %all-to-all-start.10 = ((f32[16,16,512]{2,1,0:T(8,128)}), f32[16,16,512]{2,1,0:T(8,128)S(1)}, u32[]{:S(2)}, u32[]{:S(2)}) async-start(f32[16,16,512]{2,1,0:T(8,128)} %bitcast.19), calls=%async_computation.10 | async-start | bytes 1048576 | tf_op jit(solution)/shard_map/all_to_all | solution.py:90
  259.1 13.3 %all-to-all-done.10 = f32[16,16,512]{2,1,0:T(8,128)S(1)} async-done(((f32[16,16,512]{2,1,0:T(8,128)}), f32[16,16,512]{2,1,0:T(8,128)S(1)}, u32[]{:S(2)}, u32[]{:S(2)}) %all-to-all-start.10) | async-done | bytes 524320 | tf_op jit(solution)/shard_map/all_to_all | solution.py:90
  273.2 1.1 copy.50
  274.3 6.9 %all-to-all-start.11 = ((f32[16,16,512]{2,1,0:T(8,128)}), f32[16,16,512]{2,1,0:T(8,128)S(1)}, u32[]{:S(2)}, u32[]{:S(2)}) async-start(f32[16,16,512]{2,1,0:T(8,128)} %copy.50), calls=%async_computation.11 | async-start | bytes 1048576 | tf_op jit(solution)/shard_map/all_to_all | solution.py:82
  281.2 15.7 %psum.35 = f32[]{:T(128)} all-reduce(f32[]{:T(128)} %get-tuple-element.2), channel_id=1, replica_groups=mesh['row_0'=8,'row_1'=2,'row_2'=2,'col_0'=4,'col_1'=4] {'row_0'}, use_global_device_ids=true, to_apply=%region_1.2 | all-reduce | flops 1 | bytes 8 | tf_op jit(solution)/shard_map/psum | solution.py:15
  296.9 5.5 %psum.36 = f32[]{:T(128)} all-reduce(f32[]{:T(128)} %psum.35), channel_id=1, replica_groups=mesh['row_0'=8,'row_1'=2,'row_2'=2,'col_0'=4,'col_1'=4] {'row_1'}, use_global_device_ids=true, to_apply=%region_2.3 | all-reduce | flops 1 | bytes 8 | tf_op jit(solution)/shard_map/psum | solution.py:15
  302.5 3.1 psum.37
  305.6 13.3 %psum.38 = f32[]{:T(128)} all-reduce(f32[]{:T(128)} %psum.37), channel_id=1, replica_groups=mesh['row_0'=8,'row_1'=2,'row_2'=2,'col_0'=4,'col_1'=4] {'col_0'}, use_global_device_ids=true, to_apply=%region_4.5 | all-reduce | flops 1 | bytes 8 | tf_op jit(solution)/shard_map/psum | solution.py:15
  319.5 11.0 %psum.39 = f32[]{:T(128)} all-reduce(f32[]{:T(128)} %psum.38), channel_id=1, replica_groups=mesh['row_0'=8,'row_1'=2,'row_2'=2,'col_0'=4,'col_1'=4] {'col_1'}, use_global_device_ids=true, to_apply=%region_5.6 | all-reduce | flops 1 | bytes 8 | tf_op jit(solution)/shard_map/psum | solution.py:15
  (28 shorter events, 7.8 us)
Async XLA Ops:
  31.2 20.3 %all-to-all-start.1 = ((f32[16,16,512]{2,1,0:T(8,128)}), f32[16,16,512]{2,1,0:T(8,128)S(1)}, u32[]{:S(2)}, u32[]{:S(2)}) async-start(f32[16,16,512]{2,1,0:T(8,128)} %copy.34), calls=%async_computation.1 | async-start | bytes 1048576 | tf_op jit(solution)/shard_map/all_to_all | solution.py:82
  51.5 22.6 %all-to-all-start.2 = ((f32[16,16,512]{2,1,0:T(8,128)}), f32[16,16,512]{2,1,0:T(8,128)S(1)}, u32[]{:S(2)}, u32[]{:S(2)}) async-start(f32[16,16,512]{2,1,0:T(8,128)} %copy.37), calls=%async_computation.2 | async-start | bytes 1048576 | tf_op jit(solution)/shard_map/all_to_all | solution.py:82
  108.3 21.6 %all-to-all-start.4 = ((f32[32,8,512]{2,1,0:T(8,128)}), f32[32,8,512]{2,1,0:T(8,128)S(1)}, u32[]{:S(2)}, u32[]{:S(2)}) async-start(f32[32,8,512]{2,1,0:T(8,128)} %copy.41), calls=%async_computation.4 | async-start | bytes 1048576 | tf_op jit(solution)/shard_map/all_to_all | solution.py:99
  129.9 21.9 %all-to-all-start.5 = ((f32[32,8,512]{2,1,0:T(8,128)}), f32[32,8,512]{2,1,0:T(8,128)S(1)}, u32[]{:S(2)}, u32[]{:S(2)}) async-start(f32[32,8,512]{2,1,0:T(8,128)} %copy.44), calls=%async_computation.5 | async-start | bytes 1048576 | tf_op jit(solution)/shard_map/all_to_all | solution.py:99
  157.8 22.0 %all-to-all-start.6 = ((f32[32,8,512]{2,1,0:T(8,128)}), f32[32,8,512]{2,1,0:T(8,128)S(1)}, u32[]{:S(2)}, u32[]{:S(2)}) async-start(f32[32,8,512]{2,1,0:T(8,128)} %fusion.1), calls=%async_computation.6 | async-start | bytes 1048576 | tf_op jit(solution)/shard_map/all_to_all | solution.py:107
  179.8 21.9 %all-to-all-start.7 = ((f32[32,8,512]{2,1,0:T(8,128)}), f32[32,8,512]{2,1,0:T(8,128)S(1)}, u32[]{:S(2)}, u32[]{:S(2)}) async-start(f32[32,8,512]{2,1,0:T(8,128)} %fusion), calls=%async_computation.7 | async-start | bytes 1048576 | tf_op jit(solution)/shard_map/all_to_all | solution.py:107
  230.1 21.4 %all-to-all-start.9 = ((f32[16,16,512]{2,1,0:T(8,128)}), f32[16,16,512]{2,1,0:T(8,128)S(1)}, u32[]{:S(2)}, u32[]{:S(2)}) async-start(f32[16,16,512]{2,1,0:T(8,128)} %bitcast.17), calls=%async_computation.9 | async-start | bytes 1048576 | tf_op jit(solution)/shard_map/all_to_all | solution.py:90
  251.5 20.9 %all-to-all-start.10 = ((f32[16,16,512]{2,1,0:T(8,128)}), f32[16,16,512]{2,1,0:T(8,128)S(1)}, u32[]{:S(2)}, u32[]{:S(2)}) async-start(f32[16,16,512]{2,1,0:T(8,128)} %bitcast.19), calls=%async_computation.10 | async-start | bytes 1048576 | tf_op jit(solution)/shard_map/all_to_all | solution.py:90
  274.3 56.9 %copy-start = (f32[256,512]{1,0:T(8,128)S(1)}, f32[256,512]{1,0:T(8,128)}, u32[]{:S(2)}) copy-start(f32[256,512]{1,0:T(8,128)} %param.5) | copy-start | bytes 1572868
  274.3 56.9 %all-to-all-start.11 = ((f32[16,16,512]{2,1,0:T(8,128)}), f32[16,16,512]{2,1,0:T(8,128)S(1)}, u32[]{:S(2)}, u32[]{:S(2)}) async-start(f32[16,16,512]{2,1,0:T(8,128)} %copy.50), calls=%async_computation.11 | async-start | bytes 1048576 | tf_op jit(solution)/shard_map/all_to_all | solution.py:82
where the time goes:
time: 338 us; the launch traced here: 333 us
  blocking collectives  123 us (36%)
  waiting for transfers between devices  103 us (30%)
  starting transfers between devices  52.6 us (16%)
  matrix products  42.5 us (13%)
  local copies, waits for them, and re-layouts  6.02 us (2%)
  between operations  4.34 us (1%)
    psum x5, blocking collectives, over_axes(): array = lax.psum(array, axis)  48.7 us
    all_to_all x2, waiting for transfers between devices, across_rows(): lax.all_to_all(shaped, ROW, split_axis=0, concat_axis=0, tiled=True)  29.6 us
    all_to_all x2, waiting for transfers between devices, handle(): return lax.all_to_all(mixed, ROW, split_axis=0, concat_axis=0, tiled=True)  28.9 us
    all_to_all x1, blocking collectives, across_columns(): lax.all_to_all(shaped, COL, split_axis=0, concat_axis=0, tiled=True)  28.6 us
    all_to_all x1, blocking collectives, across_rows(): lax.all_to_all(shaped, ROW, split_axis=0, concat_axis=0, tiled=True)  25.2 us
    all_to_all x2, waiting for transfers between devices, across_columns(): lax.all_to_all(shaped, COL, split_axis=0, concat_axis=0, tiled=True)  22.4 us
    all_to_all x3, waiting for transfers between devices, handle(): return lax.all_to_all(mixed, COL, split_axis=0, concat_axis=0, tiled=True)  21.6 us
    all_to_all x1, blocking collectives, handle(): return lax.all_to_all(mixed, ROW, split_axis=0, concat_axis=0, tiled=True)  21 us
  transfers between devices with their start and end apart: 9, of which 8 were waited for; matrix products, arithmetic and copies ran while one was open for 7% of the time, Pallas kernels for 0%

commit v1 on v0

--- a/solution.py
+++ b/solution.py
@@ -12,7 +12,7 @@
 
 def over_axes(array, axes):
     for axis in axes:
-        array = lax.psum(array, axis)
+        array = jnp.sum(lax.all_gather(array, axis), axis=0)
     return array
 
 

time: 338 us -> 352 us (1.041)
  local copies, waits for them, and re-layouts: 6.02 us -> 19.9 us
    psum x5 -> x0, blocking collectives: 48.7 us -> none  [over_axes(): array = lax.psum(array, axis)]
    unnamed x0 -> x5, blocking collectives: none -> 45.6 us
    unnamed x2 -> x17, local copies, waits for them, and re-layouts: 0.01 us -> 13.9 us
  transfers between devices with their start and end apart: 9 -> 9, of which waited for: 8 -> 8; matrix products, arithmetic and copies ran while one was open for 7% -> 12% of each run, Pallas kernels for 0% -> 0%
where the time goes in v1:
time: 352 us; the launch traced here: 347 us
  blocking collectives  120 us (34%)
  waiting for transfers between devices  103 us (29%)
  starting transfers between devices  52.6 us (15%)
  matrix products  42.4 us (12%)
  local copies, waits for them, and re-layouts  19.9 us (6%)
  other arithmetic  5.04 us (1%)
  between operations  4.36 us (1%)
    unnamed x5, blocking collectives  45.6 us
    all_to_all x2, waiting for transfers between devices, across_rows(): lax.all_to_all(shaped, ROW, split_axis=0, concat_axis=0, tiled=True)  29.7 us
    all_to_all x2, waiting for transfers between devices, handle(): return lax.all_to_all(mixed, ROW, split_axis=0, concat_axis=0, tiled=True)  28.9 us
    all_to_all x1, blocking collectives, across_columns(): lax.all_to_all(shaped, COL, split_axis=0, concat_axis=0, tiled=True)  28.6 us
    all_to_all x1, blocking collectives, across_rows(): lax.all_to_all(shaped, ROW, split_axis=0, concat_axis=0, tiled=True)  25.2 us
    all_to_all x2, waiting for transfers between devices, across_columns(): lax.all_to_all(shaped, COL, split_axis=0, concat_axis=0, tiled=True)  22.4 us
    all_to_all x3, waiting for transfers between devices, handle(): return lax.all_to_all(mixed, COL, split_axis=0, concat_axis=0, tiled=True)  21.6 us
    all_to_all x1, blocking collectives, handle(): return lax.all_to_all(mixed, ROW, split_axis=0, concat_axis=0, tiled=True)  21 us
  transfers between devices with their start and end apart: 9, of which 8 were waited for; matrix products, arithmetic and copies ran while one was open for 12% of the time, Pallas kernels for 0%

profile of v1, /device:TPU:8, one launch (start us, length us, event | category | flops | bytes accessed | tf_op | source)
XLA Modules:
  0.0 347.3 jit_solution(6164134636935028108)
XLA Ops:
  0.6 28.6 %all_to_all.60 = f32[16,16,512]{2,1,0:T(8,128)S(1)} all-to-all(f32[16,16,512]{2,1,0:T(8,128)} %bitcast.67), channel_id=1, replica_groups=mesh['row_0'=8,'row_1'=2,'row_2'=2,'col_0'=4,'col_1'=4] {'col_0','col_1'}, dimensions={0} | all-to-all | bytes 1048576 | tf_op jit(solution)/shard_map/all_to_all | solution.py:90
  30.1 1.1 copy.34
  31.2 5.9 %all-to-all-start.1 = ((f32[16,16,512]{2,1,0:T(8,128)}), f32[16,16,512]{2,1,0:T(8,128)S(1)}, u32[]{:S(2)}, u32[]{:S(2)}) async-start(f32[16,16,512]{2,1,0:T(8,128)} %copy.34), calls=%async_computation.1 | async-start | bytes 1048576 | tf_op jit(solution)/shard_map/all_to_all | solution.py:82
  39.1 12.4 %all-to-all-done.1 = f32[16,16,512]{2,1,0:T(8,128)S(1)} async-done(((f32[16,16,512]{2,1,0:T(8,128)}), f32[16,16,512]{2,1,0:T(8,128)S(1)}, u32[]{:S(2)}, u32[]{:S(2)}) %all-to-all-start.1) | async-done | bytes 524320 | tf_op jit(solution)/shard_map/all_to_all | solution.py:82
  51.5 7.4 %all-to-all-start.2 = ((f32[16,16,512]{2,1,0:T(8,128)}), f32[16,16,512]{2,1,0:T(8,128)S(1)}, u32[]{:S(2)}, u32[]{:S(2)}) async-start(f32[16,16,512]{2,1,0:T(8,128)} %copy.37), calls=%async_computation.2 | async-start | bytes 1048576 | tf_op jit(solution)/shard_map/all_to_all | solution.py:82
  58.9 3.0 fusion.33
  61.9 2.9 fusion.30
  64.9 9.2 %all-to-all-done.2 = f32[16,16,512]{2,1,0:T(8,128)S(1)} async-done(((f32[16,16,512]{2,1,0:T(8,128)}), f32[16,16,512]{2,1,0:T(8,128)S(1)}, u32[]{:S(2)}, u32[]{:S(2)}) %all-to-all-start.2) | async-done | bytes 524320 | tf_op jit(solution)/shard_map/all_to_all | solution.py:82
  74.1 3.1 convolution_add_fusion.8
  77.2 3.6 %convolution_add_fusion.9 = f32[256,256]{0,1:T(8,128)S(1)} fusion(f32[256,256]{0,1:T(8,128)S(1)} %fusion.30, f32[256,512]{1,0:T(8,128)S(1)} %bitcast.71, f32[]{:T(128)S(6)} %neg.6, s32[512]{0:T(512)S(1)} %multiply_add_fusion, s32[256]{0:T(256)S(1)} %get-tuple-element.5, f32[256]{0:T(256)S(1)} %compare_select_fusion.4), kind=kOutput, calls=%fused_computation.11 | convolution fusion | flops 404815872 | bytes 1052676 | tf_op jit(solution)/shard_map/dot_general | solution.py:125
  81.0 25.2 %all_to_all.61 = f32[32,8,512]{2,1,0:T(8,128)S(1)} all-to-all(f32[32,8,512]{2,1,0:T(8,128)S(1)} %bitcast.66), channel_id=1, replica_groups=mesh['row_0'=8,'row_1'=2,'row_2'=2,'col_0'=4,'col_1'=4] {'row_0','row_1'..., dimensions={0} | all-to-all | bytes 1048576 | tf_op jit(solution)/shard_map/all_to_all | solution.py:107
  108.3 4.7 %all-to-all-start.4 = ((f32[32,8,512]{2,1,0:T(8,128)}), f32[32,8,512]{2,1,0:T(8,128)S(1)}, u32[]{:S(2)}, u32[]{:S(2)}) async-start(f32[32,8,512]{2,1,0:T(8,128)} %copy.41), calls=%async_computation.4 | async-start | bytes 1048576 | tf_op jit(solution)/shard_map/all_to_all | solution.py:99
  115.7 14.1 %all-to-all-done.4 = f32[32,8,512]{2,1,0:T(8,128)S(1)} async-done(((f32[32,8,512]{2,1,0:T(8,128)}), f32[32,8,512]{2,1,0:T(8,128)S(1)}, u32[]{:S(2)}, u32[]{:S(2)}) %all-to-all-start.4) | async-done | bytes 524320 | tf_op jit(solution)/shard_map/all_to_all | solution.py:99
  129.9 5.0 %all-to-all-start.5 = ((f32[32,8,512]{2,1,0:T(8,128)}), f32[32,8,512]{2,1,0:T(8,128)S(1)}, u32[]{:S(2)}, u32[]{:S(2)}) async-start(f32[32,8,512]{2,1,0:T(8,128)} %copy.44), calls=%async_computation.5 | async-start | bytes 1048576 | tf_op jit(solution)/shard_map/all_to_all | solution.py:99
  137.0 14.7 %all-to-all-done.5 = f32[32,8,512]{2,1,0:T(8,128)S(1)} async-done(((f32[32,8,512]{2,1,0:T(8,128)}), f32[32,8,512]{2,1,0:T(8,128)S(1)}, u32[]{:S(2)}, u32[]{:S(2)}) %all-to-all-start.5) | async-done | bytes 524320 | tf_op jit(solution)/shard_map/all_to_all | solution.py:99
  154.8 1.1 fusion.65
  155.9 1.9 fusion.1
  157.8 5.3 %all-to-all-start.6 = ((f32[32,8,512]{2,1,0:T(8,128)}), f32[32,8,512]{2,1,0:T(8,128)S(1)}, u32[]{:S(2)}, u32[]{:S(2)}) async-start(f32[32,8,512]{2,1,0:T(8,128)} %fusion.1), calls=%async_computation.6 | async-start | bytes 1048576 | tf_op jit(solution)/shard_map/all_to_all | solution.py:107
  163.1 1.1 fusion.63
  164.2 2.0 fusion
  166.2 13.7 %all-to-all-done.6 = f32[32,8,512]{2,1,0:T(8,128)S(1)} async-done(((f32[32,8,512]{2,1,0:T(8,128)}), f32[32,8,512]{2,1,0:T(8,128)S(1)}, u32[]{:S(2)}, u32[]{:S(2)}) %all-to-all-start.6) | async-done | bytes 524320 | tf_op jit(solution)/shard_map/all_to_all | solution.py:107
  179.8 5.0 %all-to-all-start.7 = ((f32[32,8,512]{2,1,0:T(8,128)}), f32[32,8,512]{2,1,0:T(8,128)S(1)}, u32[]{:S(2)}, u32[]{:S(2)}) async-start(f32[32,8,512]{2,1,0:T(8,128)} %fusion), calls=%async_computation.7 | async-start | bytes 1048576 | tf_op jit(solution)/shard_map/all_to_all | solution.py:107
  185.7 16.0 %all-to-all-done.7 = f32[32,8,512]{2,1,0:T(8,128)S(1)} async-done(((f32[32,8,512]{2,1,0:T(8,128)}), f32[32,8,512]{2,1,0:T(8,128)S(1)}, u32[]{:S(2)}, u32[]{:S(2)}) %all-to-all-start.7) | async-done | bytes 524320 | tf_op jit(solution)/shard_map/all_to_all | solution.py:107
  203.0 21.0 %all_to_all.62 = f32[32,8,512]{2,1,0:T(8,128)S(1)} all-to-all(f32[32,8,512]{2,1,0:T(8,128)S(1)} %copy.47), channel_id=1, replica_groups=mesh['row_0'=8,'row_1'=2,'row_2'=2,'col_0'=4,'col_1'=4] {'row_0','row_1'..., dimensions={0} | all-to-all | bytes 1048576 | tf_op jit(solution)/shard_map/all_to_all | solution.py:99
  223.9 2.6 fusion.29
  226.5 3.6 %convolution_add_fusion.5 = f32[256,512]{1,0:T(8,128)} fusion(f32[256,512]{1,0:T(8,128)S(1)} %fusion.29, f32[256]{0:T(256)S(1)} %compare_select_fusion.2, f32[]{:T(128)S(6)} %convert_element_type.56, s32[256]{0:T(256)S(1)} %get-tuple-element.4, s32[512]{0:T(512)S(1)} %multiply_add_fusion, f32[256,512]{1,0:T(8,128)S(1)} %bitcast.73), kind=kOutput, calls=%fused_computation.7 | convolution fusion | flops 404881408 | bytes 1314820 | tf_op jit(solution)/shard_map/dot_general | solution.py:158
  230.1 5.8 %all-to-all-start.9 = ((f32[16,16,512]{2,1,0:T(8,128)}), f32[16,16,512]{2,1,0:T(8,128)S(1)}, u32[]{:S(2)}, u32[]{:S(2)}) async-start(f32[16,16,512]{2,1,0:T(8,128)} %bitcast.17), calls=%async_computation.9 | async-start | bytes 1048576 | tf_op jit(solution)/shard_map/all_to_all | solution.py:90
  235.9 2.6 fusion.31
  238.6 3.8 %convolution_add_fusion.4 = f32[256,512]{1,0:T(8,128)} fusion(f32[256,512]{1,0:T(8,128)S(1)} %fusion.31, f32[256]{0:T(256)S(1)} %compare_select_fusion.2, s32[256]{0:T(256)S(1)} %get-tuple-element.4, s32[512]{0:T(512)S(1)} %multiply_add_fusion, pred[]{:T(512)S(6)} %gt.32, f32[256,512]{1,0:T(8,128)S(1)} %bitcast.75), kind=kOutput, calls=%fused_computation.6 | convolution fusion | flops 405012480 | bytes 1314817 | tf_op jit(solution)/shard_map/dot_general | solution.py:161
  242.3 9.2 %all-to-all-done.9 = f32[16,16,512]{2,1,0:T(8,128)S(1)} async-done(((f32[16,16,512]{2,1,0:T(8,128)}), f32[16,16,512]{2,1,0:T(8,128)S(1)}, u32[]{:S(2)}, u32[]{:S(2)}) %all-to-all-start.9) | async-done | bytes 524320 | tf_op jit(solution)/shard_map/all_to_all | solution.py:90
  251.5 6.7 %all-to-all-start.10 = ((f32[16,16,512]{2,1,0:T(8,128)}), f32[16,16,512]{2,1,0:T(8,128)S(1)}, u32[]{:S(2)}, u32[]{:S(2)}) async-start(f32[16,16,512]{2,1,0:T(8,128)} %bitcast.19), calls=%async_computation.10 | async-start | bytes 1048576 | tf_op jit(solution)/shard_map/all_to_all | solution.py:90
  259.1 13.2 %all-to-all-done.10 = f32[16,16,512]{2,1,0:T(8,128)S(1)} async-done(((f32[16,16,512]{2,1,0:T(8,128)}), f32[16,16,512]{2,1,0:T(8,128)S(1)}, u32[]{:S(2)}, u32[]{:S(2)}) %all-to-all-start.10) | async-done | bytes 524320 | tf_op jit(solution)/shard_map/all_to_all | solution.py:90
  274.2 6.9 %all-to-all-start.11 = ((f32[16,16,512]{2,1,0:T(8,128)}), f32[16,16,512]{2,1,0:T(8,128)S(1)}, u32[]{:S(2)}, u32[]{:S(2)}) async-start(f32[16,16,512]{2,1,0:T(8,128)} %copy.50), calls=%async_computation.11 | async-start | bytes 1048576 | tf_op jit(solution)/shard_map/all_to_all | solution.py:82
  281.2 1.3 dynamic-slice
  282.5 1.4 dynamic-update-slice
  283.9 1.3 dynamic-slice.1
  285.3 15.2 %all-reduce = f32[8]{0:T(128)S(1)} all-reduce(f32[8]{0:T(128)S(1)} %dynamic-update-slice), channel_id=1, replica_groups=mesh['row_0'=8,'row_1'=2,'row_2'=2,'col_0'=4,'col_1'=4] {'row_0'}, use_global_device_ids=true, to_apply=%add | all-reduce | flops 8 | bytes 64
  301.1 1.4 dynamic-update-slice.1
  302.6 1.3 dynamic-slice.2
  303.9 4.9 %all-reduce.1 = f32[2]{0:T(128)S(1)} all-reduce(f32[2]{0:T(128)S(1)} %dynamic-update-slice.1), channel_id=1, replica_groups=mesh['row_0'=8,'row_1'=2,'row_2'=2,'col_0'=4,'col_1'=4] {'row_1'}, use_global_device_ids=true, to_apply=%add.1 | all-reduce | flops 2 | bytes 16
  309.4 1.4 dynamic-update-slice.2
  310.9 1.3 dynamic-slice.3
  312.2 2.4 all-reduce.2
  315.3 1.4 dynamic-update-slice.3
  316.7 1.3 dynamic-slice.4
  318.0 12.6 %all-reduce.3 = f32[4]{0:T(128)S(1)} all-reduce(f32[4]{0:T(128)S(1)} %dynamic-update-slice.3), channel_id=1, replica_groups=mesh['row_0'=8,'row_1'=2,'row_2'=2,'col_0'=4,'col_1'=4] {'col_0'}, use_global_device_ids=true, to_apply=%add.3 | all-reduce | flops 4 | bytes 32
  331.3 1.4 dynamic-update-slice.4
  333.4 10.4 %all-reduce.4 = f32[4]{0:T(128)S(1)} all-reduce(f32[4]{0:T(128)S(1)} %dynamic-update-slice.4), channel_id=1, replica_groups=mesh['row_0'=8,'row_1'=2,'row_2'=2,'col_0'=4,'col_1'=4] {'col_1'}, use_global_device_ids=true, to_apply=%add.4 | all-reduce | flops 4 | bytes 32
  (48 shorter events, 21.1 us)
Async XLA Ops:
  31.2 20.3 %all-to-all-start.1 = ((f32[16,16,512]{2,1,0:T(8,128)}), f32[16,16,512]{2,1,0:T(8,128)S(1)}, u32[]{:S(2)}, u32[]{:S(2)}) async-start(f32[16,16,512]{2,1,0:T(8,128)} %copy.34), calls=%async_computation.1 | async-start | bytes 1048576 | tf_op jit(solution)/shard_map/all_to_all | solution.py:82
  51.5 22.6 %all-to-all-start.2 = ((f32[16,16,512]{2,1,0:T(8,128)}), f32[16,16,512]{2,1,0:T(8,128)S(1)}, u32[]{:S(2)}, u32[]{:S(2)}) async-start(f32[16,16,512]{2,1,0:T(8,128)} %copy.37), calls=%async_computation.2 | async-start | bytes 1048576 | tf_op jit(solution)/shard_map/all_to_all | solution.py:82
  108.3 21.6 %all-to-all-start.4 = ((f32[32,8,512]{2,1,0:T(8,128)}), f32[32,8,512]{2,1,0:T(8,128)S(1)}, u32[]{:S(2)}, u32[]{:S(2)}) async-start(f32[32,8,512]{2,1,0:T(8,128)} %copy.41), calls=%async_computation.4 | async-start | bytes 1048576 | tf_op jit(solution)/shard_map/all_to_all | solution.py:99
  129.9 21.9 %all-to-all-start.5 = ((f32[32,8,512]{2,1,0:T(8,128)}), f32[32,8,512]{2,1,0:T(8,128)S(1)}, u32[]{:S(2)}, u32[]{:S(2)}) async-start(f32[32,8,512]{2,1,0:T(8,128)} %copy.44), calls=%async_computation.5 | async-start | bytes 1048576 | tf_op jit(solution)/shard_map/all_to_all | solution.py:99
  157.8 22.0 %all-to-all-start.6 = ((f32[32,8,512]{2,1,0:T(8,128)}), f32[32,8,512]{2,1,0:T(8,128)S(1)}, u32[]{:S(2)}, u32[]{:S(2)}) async-start(f32[32,8,512]{2,1,0:T(8,128)} %fusion.1), calls=%async_computation.6 | async-start | bytes 1048576 | tf_op jit(solution)/shard_map/all_to_all | solution.py:107
  179.8 21.9 %all-to-all-start.7 = ((f32[32,8,512]{2,1,0:T(8,128)}), f32[32,8,512]{2,1,0:T(8,128)S(1)}, u32[]{:S(2)}, u32[]{:S(2)}) async-start(f32[32,8,512]{2,1,0:T(8,128)} %fusion), calls=%async_computation.7 | async-start | bytes 1048576 | tf_op jit(solution)/shard_map/all_to_all | solution.py:107
  230.1 21.4 %all-to-all-start.9 = ((f32[16,16,512]{2,1,0:T(8,128)}), f32[16,16,512]{2,1,0:T(8,128)S(1)}, u32[]{:S(2)}, u32[]{:S(2)}) async-start(f32[16,16,512]{2,1,0:T(8,128)} %bitcast.17), calls=%async_computation.9 | async-start | bytes 1048576 | tf_op jit(solution)/shard_map/all_to_all | solution.py:90
  251.5 20.7 %all-to-all-start.10 = ((f32[16,16,512]{2,1,0:T(8,128)}), f32[16,16,512]{2,1,0:T(8,128)S(1)}, u32[]{:S(2)}, u32[]{:S(2)}) async-start(f32[16,16,512]{2,1,0:T(8,128)} %bitcast.19), calls=%async_computation.10 | async-start | bytes 1048576 | tf_op jit(solution)/shard_map/all_to_all | solution.py:90
  274.2 70.8 %copy-start = (f32[256,512]{1,0:T(8,128)S(1)}, f32[256,512]{1,0:T(8,128)}, u32[]{:S(2)}) copy-start(f32[256,512]{1,0:T(8,128)} %param.5) | copy-start | bytes 1572868
  274.2 70.8 %all-to-all-start.11 = ((f32[16,16,512]{2,1,0:T(8,128)}), f32[16,16,512]{2,1,0:T(8,128)S(1)}, u32[]{:S(2)}, u32[]{:S(2)}) async-start(f32[16,16,512]{2,1,0:T(8,128)} %copy.50), calls=%async_computation.11 | async-start | bytes 1048576 | tf_op jit(solution)/shard_map/all_to_all | solution.py:82
